TPU v7x, 32 devices: a whole 2x2x4 slice. The times are simulated.
32 devices in a mesh: tm: 8 (over z, x), chan: 4 (over y, core).
Axes of the slice: x: 2, y: 2, z: 4, core: 2. Of those that a mesh axis runs over, the one named last changes fastest.
Arguments:
- surveillance: bfloat16 [128, 1024, 256], P(('chan', 'tm')), parts along dimension 0, may hold values from -6 to 6
- ref_samples: bfloat16 [32, 1040, 256], P('tm'), may hold values from -6 to 6
- block_ids: int32 [32], P('tm'), may hold values from 0 to 31, each once
- walk: int32 [32], P('tm'), may hold values from 0 to 63
- cfar_guard: int32 [2048], P('tm'), may hold values from 1 to 8
- cfar_window: int32 [2048], P('tm'), may hold values from 1 to 16
Outputs:
- detection: float32 [8192, 512], P(('chan', 'tm')), parts along dimension 0
There are 4 independent parts, one for each index of `chan`. A program takes and returns all parts, laid end to end along the dimension named above; an argument that names none is the same for every part. Nothing has to cross between parts.
Inputs may be any that keep to these rules, and one draw needn't show every extreme that they name: block_ids names each of 0 to 31 exactly once.
All inputs are finite; a program needn't handle non-finite values.
Results may differ from a plain program's by a relative error of at most 0.0003.
Values sent between devices are 32-bit elements; how exact they have to be, the bound alone decides.
No kernel may reach another device: no remote copies, remote signals or barrier semaphores. Data moves between devices by JAX's collectives and lax.ppermute only.
A program may use at most 64 MiB of HBM per device.

v0:
```python
import math

import jax
import jax.numpy as jnp
from jax import lax
from jax.sharding import PartitionSpec as P

D = 2048
DOP = 512
SEGS = 64
GUARD_MAX = 8
WIN_MAX = 16


HIGH = lax.Precision.HIGHEST


def with_halo(x, sides, width):
    for axis, dim in sides:
        count, length = (lax.axis_size(axis), x.shape[dim])
        up = [(i, (i + 1) % count) for i in range(count - 1)]
        down = [(j, i) for i, j in up]
        last = lax.slice_in_dim(x, length - width, length, axis=dim)
        initial = lax.slice_in_dim(x, 0, width, axis=dim)
        before = lax.ppermute(last, axis, up)
        after = lax.ppermute(initial, axis, down)
        x = jnp.concatenate([before, x, after], axis=dim)
    return x


def phase(product, total):
    return 2.0 * math.pi / total * (product % total).astype(jnp.float32)


def square_tables(width):
    place = jnp.arange(width, dtype=jnp.int32)
    theta = phase(place[:, None] * place[None, :], width)
    return (jnp.cos(theta), jnp.sin(theta))


def make_tables():
    length = 2 * D
    rows = length // 128
    small_cos, small_sin = square_tables(rows)
    wide_cos, wide_sin = square_tables(128)
    mixer = jnp.concatenate(
        [jnp.concatenate([wide_cos, -wide_sin], 1), jnp.concatenate([wide_sin, wide_cos], 1)], 0
    )
    first_idx = jnp.arange(rows, dtype=jnp.int32)[:, None]
    second_idx = jnp.arange(128, dtype=jnp.int32)[None, :]
    twist = phase(first_idx * second_idx, length)
    spread = first_idx + rows * second_idx
    return (small_cos, small_sin, jnp.cos(twist), jnp.sin(twist), mixer, spread)


def forward(signal, tables):
    small_cos, small_sin, twist_cos, twist_sin, mixer, spread = tables
    first = jnp.einsum("kn,snc->skc", small_cos, signal, precision=HIGH)
    second = jnp.einsum("kn,snc->skc", small_sin, signal, precision=HIGH)
    real_part = first[..., :128] + second[..., 128:]
    imag_part = first[..., 128:] - second[..., :128]
    turned = jnp.concatenate(
        [
            real_part * twist_cos + imag_part * twist_sin,
            imag_part * twist_cos - real_part * twist_sin,
        ],
        axis=-1,
    )
    return jnp.einsum("skc,cd->skd", turned, mixer, precision=HIGH)


def inverse(spectrum, tables):
    small_cos, small_sin, twist_cos, twist_sin, mixer, spread = tables
    mixed = jnp.dot(spectrum, mixer.T, precision=HIGH)
    real_part = mixed[:, :128]
    imag_part = mixed[:, 128:]
    turned = jnp.concatenate(
        [
            real_part * twist_cos - imag_part * twist_sin,
            imag_part * twist_cos + real_part * twist_sin,
        ],
        axis=-1,
    )
    with_cos = jnp.dot(small_cos, turned, precision=HIGH)
    with_sin = jnp.dot(small_sin, turned, precision=HIGH)
    result = jnp.concatenate(
        [with_cos[:, :128] - with_sin[:, 128:], with_cos[:, 128:] + with_sin[:, :128]], axis=-1
    )
    return result / (2.0 * D)


def correlate(surv_rows, ref_rows, shift, tables):
    seg_rows = D // 128
    rows_all = surv_rows.shape[0]
    segs = rows_all // seg_rows
    echo = surv_rows.astype(jnp.float32).reshape(segs, seg_rows, 256)
    echo = jnp.concatenate([echo, jnp.zeros_like(echo)], axis=1)
    direct = ref_rows.astype(jnp.float32)
    direct = jnp.concatenate(
        [
            direct[:rows_all].reshape(segs, seg_rows, 256),
            direct[seg_rows:].reshape(segs, seg_rows, 256),
        ],
        axis=1,
    )
    echo_hat = forward(echo, tables)
    direct_hat = forward(direct, tables)
    echo_re = echo_hat[..., :128]
    echo_im = echo_hat[..., 128:]
    direct_re = direct_hat[..., :128]
    direct_im = direct_hat[..., 128:]
    spec_re = jnp.sum(echo_re * direct_re + echo_im * direct_im, axis=0)
    spec_im = jnp.sum(echo_im * direct_re - echo_re * direct_im, axis=0)
    ramp = phase(tables[5] * shift, 2 * D)
    ramp_cos = jnp.cos(ramp)
    ramp_sin = jnp.sin(ramp)
    turned = jnp.concatenate(
        [spec_re * ramp_cos + spec_im * ramp_sin, spec_im * ramp_cos - spec_re * ramp_sin], axis=-1
    )
    lagged = inverse(turned, tables)
    picked = lagged[seg_rows:]
    delay_idx = (
        128 * jnp.arange(seg_rows, dtype=jnp.int32)[:, None]
        + (jnp.arange(256, dtype=jnp.int32) % 128)[None, :]
    )
    return jnp.where(delay_idx >= shift, picked, 0.0)


def doppler_mixer(ids, norm):
    freq = jnp.arange(DOP, dtype=jnp.int32)
    theta = phase(ids[:, None] * freq[None, :], DOP)
    cos_table = jnp.cos(theta) * norm
    sin_table = jnp.sin(theta) * norm
    return jnp.concatenate(
        [jnp.concatenate([cos_table, -sin_table], 1), jnp.concatenate([sin_table, cos_table], 1)], 0
    )


def body(surveillance, ref_samples, block_ids, walk, cfar_guard, cfar_window):
    blocks = surveillance.shape[0]
    devices = lax.axis_size("tm")
    total_blocks = blocks * devices
    span = D // devices
    reach = GUARD_MAX + WIN_MAX
    base = lax.axis_index("tm") * span
    tables = make_tables()
    corr = lax.map(
        lambda item: correlate(item[0], item[1], item[2], tables), (surveillance, ref_samples, walk)
    )
    real_c = corr[:, :, :128].reshape(blocks, D)
    imag_c = corr[:, :, 128:].reshape(blocks, D)
    norm = 1.0 / math.sqrt(total_blocks * SEGS * D)
    moved = lax.all_to_all(
        jnp.stack([real_c, imag_c], axis=1), "tm", split_axis=2, concat_axis=0, tiled=True
    )
    ids = lax.all_gather(block_ids, "tm", axis=0, tiled=True)
    stacked = jnp.concatenate([moved[:, 0], moved[:, 1]], 0)
    mixer = doppler_mixer(ids, norm)
    amp = lax.dot_general(stacked, mixer, (((0,), (0,)), ((), ())), precision=HIGH)
    floor = jnp.sum(moved * moved, axis=(0, 1))
    floor = floor / (total_blocks * SEGS * D)
    power = amp[:, :DOP] * amp[:, :DOP] + amp[:, DOP:] * amp[:, DOP:]
    padded = with_halo(power, (("tm", 0),), reach)
    guard = cfar_guard[:, None]
    width = cfar_window[:, None]

    def inside(dist):
        return ((dist > guard) & (dist <= guard + width)).astype(jnp.float32)

    row_idx = jnp.arange(span, dtype=jnp.int32)[:, None]
    col_idx = jnp.arange(span + 2 * reach, dtype=jnp.int32)[None, :]
    band = inside(jnp.abs(col_idx - reach - row_idx))
    spot = base + jnp.arange(span + 2 * reach, dtype=jnp.int32) - reach
    valid = ((spot >= 0) & (spot < D)).astype(jnp.float32)
    delay_sum = jnp.dot(band, padded, precision=HIGH)
    count = jnp.dot(band, valid, precision=HIGH)
    doppler_sum = jnp.zeros_like(power)
    for step in range(1, reach + 1):
        active = inside(jnp.full((1, 1), step, jnp.int32))
        doppler_sum = doppler_sum + active * (
            jnp.roll(power, -step, axis=1) + jnp.roll(power, step, axis=1)
        )
    noise = (delay_sum + doppler_sum) / (count[:, None] + 2.0 * width.astype(jnp.float32))
    return (power - floor[:, None]) / (0.25 + noise)


def solution(mesh):
    in_specs = (
        P(("chan", "tm"), None, None),
        P("tm", None, None),
        P("tm"),
        P("tm"),
        P("tm"),
        P("tm"),
    )
    out_specs = P(("chan", "tm"), None)
    return jax.shard_map(body, mesh=mesh, in_specs=in_specs, out_specs=out_specs, check_vma=False)
```

profile of v0, /device:TPU:0, one launch (start us, length us, event | category | flops | bytes accessed | tf_op | source)
XLA Modules:
  0.0 126.7 jit_solution(17962002947929078072)
XLA Ops:
  0.6 69.0 %while.15 = (s32[]{:T(128)}, f32[4,16,256]{2,1,0:T(8,128)S(1)}, s32[4]{0:T(128)}, bf16[4,1024,256]{2,1,0:T(8,128)(2,1)}, f32[256,256]{1,0:T(8,128)S(1)}, /*index...) while((s32[]{:T(128)}, f32[4,16,256]{2,1,0:T(8,128)S(1)}, s32[4]{0:T(128)}, ...), condition=%wide.region_3.4_spmd.clone.clone, body=%wide.region_0.3_spmd.clone.clone.sunk | while | flops 4067001856 | bytes 47000764 | solution.py:147
  0.6 1.3 %dynamic_slice.37 = s32[1]{0:T(128)} dynamic-slice(s32[4]{0:T(128)} %get-tuple-element.542, s32[]{:T(128)S(6)} %copy.37), dynamic_slice_sizes={1} | dynamic-slice | bytes 12 | tf_op jit(solution)/shard_map/while/body/jit(dynamic_index_in_dim)/dynamic_slice | solution.py:147
  2.0 1.1 constant_dynamic-slice_fusion.2
  3.1 1.1 dynamic-slice_convert_fusion.2
  4.4 2.0 %fusion.285 = f32[64,32,256]{2,1,0:T(8,128)S(1)} fusion(f32[64,16,256]{2,1,0:T(8,128)S(1)} %bitcast.89, f32[64,16,256]{2,1,0:T(8,128)S(1)} %bitcast.87), kind=kOutput, calls=%fused_computation.16.clone.1 | convolution fusion | flops 201865216 | bytes 4194304 | tf_op jit(solution)/shard_map/while/body/eval_jaxpr/kn,snc->skc/dot_general | solution.py:58
  6.4 2.0 %fusion.284 = f32[64,32,256]{2,1,0:T(8,128)S(1)} fusion(f32[64,16,256]{2,1,0:T(8,128)S(1)} %bitcast.90, f32[64,16,256]{2,1,0:T(8,128)S(1)} %bitcast.88), kind=kOutput, calls=%fused_computation.17.clone.1 | convolution fusion | flops 201865216 | bytes 4194304 | tf_op jit(solution)/shard_map/while/body/eval_jaxpr/kn,snc->skc/dot_general | solution.py:59
  8.4 1.0 convolution_bitcast_fusion.9
  9.5 1.0 convolution_bitcast_fusion.8
  10.5 0.8 multiply_add_fusion.7
  11.3 1.9 %fusion.286 = f32[64,32,256]{2,1,0:T(8,128)S(1)} fusion(f32[64,32,128]{2,1,0:T(8,128)S(1)} %get-tuple-element.512, f32[64,32,128]{2,1,0:T(8,128)S(1)} %get-tuple-element.513, f32[256,256]{1,0:T(8,128)S(1)} %get-tuple-element.544), kind=kOutput, calls=%fused_computation.10.clone.1 | convolution fusion | flops 1611137024 | bytes 4456448 | tf_op jit(solution)/shard_map/while/body/eval_jaxpr/skc,cd->skd/dot_general | solution.py:69
  13.2 1.9 %fusion.287 = f32[64,32,256]{2,1,0:T(8,128)S(1)} fusion(f32[64,32,128]{2,1,0:T(8,128)S(1)} %get-tuple-element.514, f32[64,32,128]{2,1,0:T(8,128)S(1)} %get-tuple-element.515, f32[256,256]{1,0:T(8,128)S(1)} %get-tuple-element.544), kind=kOutput, calls=%fused_computation.5.clone.1 | convolution fusion | flops 1611137024 | bytes 4456448 | tf_op jit(solution)/shard_map/while/body/eval_jaxpr/skc,cd->skd/dot_general | solution.py:69
  15.4 0.8 multiply_add_fusion.8
  17.1 0.7 fusion.289
  17.8 1.3 %dynamic_slice.37 = s32[1]{0:T(128)} dynamic-slice(s32[4]{0:T(128)} %get-tuple-element.542, s32[]{:T(128)S(6)} %copy.37), dynamic_slice_sizes={1} | dynamic-slice | bytes 12 | tf_op jit(solution)/shard_map/while/body/jit(dynamic_index_in_dim)/dynamic_slice | solution.py:147
  19.2 1.1 constant_dynamic-slice_fusion.2
  20.3 1.1 dynamic-slice_convert_fusion.2
  21.6 2.0 %fusion.285 = f32[64,32,256]{2,1,0:T(8,128)S(1)} fusion(f32[64,16,256]{2,1,0:T(8,128)S(1)} %bitcast.89, f32[64,16,256]{2,1,0:T(8,128)S(1)} %bitcast.87), kind=kOutput, calls=%fused_computation.16.clone.1 | convolution fusion | flops 201865216 | bytes 4194304 | tf_op jit(solution)/shard_map/while/body/eval_jaxpr/kn,snc->skc/dot_general | solution.py:58
  23.6 2.0 %fusion.284 = f32[64,32,256]{2,1,0:T(8,128)S(1)} fusion(f32[64,16,256]{2,1,0:T(8,128)S(1)} %bitcast.90, f32[64,16,256]{2,1,0:T(8,128)S(1)} %bitcast.88), kind=kOutput, calls=%fused_computation.17.clone.1 | convolution fusion | flops 201865216 | bytes 4194304 | tf_op jit(solution)/shard_map/while/body/eval_jaxpr/kn,snc->skc/dot_general | solution.py:59
  25.7 1.0 convolution_bitcast_fusion.9
  26.7 1.0 convolution_bitcast_fusion.8
  27.8 0.8 multiply_add_fusion.7
  28.5 1.9 %fusion.286 = f32[64,32,256]{2,1,0:T(8,128)S(1)} fusion(f32[64,32,128]{2,1,0:T(8,128)S(1)} %get-tuple-element.512, f32[64,32,128]{2,1,0:T(8,128)S(1)} %get-tuple-element.513, f32[256,256]{1,0:T(8,128)S(1)} %get-tuple-element.544), kind=kOutput, calls=%fused_computation.10.clone.1 | convolution fusion | flops 1611137024 | bytes 4456448 | tf_op jit(solution)/shard_map/while/body/eval_jaxpr/skc,cd->skd/dot_general | solution.py:69
  30.4 1.9 %fusion.287 = f32[64,32,256]{2,1,0:T(8,128)S(1)} fusion(f32[64,32,128]{2,1,0:T(8,128)S(1)} %get-tuple-element.514, f32[64,32,128]{2,1,0:T(8,128)S(1)} %get-tuple-element.515, f32[256,256]{1,0:T(8,128)S(1)} %get-tuple-element.544), kind=kOutput, calls=%fused_computation.5.clone.1 | convolution fusion | flops 1611137024 | bytes 4456448 | tf_op jit(solution)/shard_map/while/body/eval_jaxpr/skc,cd->skd/dot_general | solution.py:69
  32.6 0.8 multiply_add_fusion.8
  34.3 0.7 fusion.289
  35.1 1.3 %dynamic_slice.37 = s32[1]{0:T(128)} dynamic-slice(s32[4]{0:T(128)} %get-tuple-element.542, s32[]{:T(128)S(6)} %copy.37), dynamic_slice_sizes={1} | dynamic-slice | bytes 12 | tf_op jit(solution)/shard_map/while/body/jit(dynamic_index_in_dim)/dynamic_slice | solution.py:147
  36.5 1.1 constant_dynamic-slice_fusion.2
  37.6 1.1 dynamic-slice_convert_fusion.2
  38.9 2.0 %fusion.285 = f32[64,32,256]{2,1,0:T(8,128)S(1)} fusion(f32[64,16,256]{2,1,0:T(8,128)S(1)} %bitcast.89, f32[64,16,256]{2,1,0:T(8,128)S(1)} %bitcast.87), kind=kOutput, calls=%fused_computation.16.clone.1 | convolution fusion | flops 201865216 | bytes 4194304 | tf_op jit(solution)/shard_map/while/body/eval_jaxpr/kn,snc->skc/dot_general | solution.py:58
  40.9 2.0 %fusion.284 = f32[64,32,256]{2,1,0:T(8,128)S(1)} fusion(f32[64,16,256]{2,1,0:T(8,128)S(1)} %bitcast.90, f32[64,16,256]{2,1,0:T(8,128)S(1)} %bitcast.88), kind=kOutput, calls=%fused_computation.17.clone.1 | convolution fusion | flops 201865216 | bytes 4194304 | tf_op jit(solution)/shard_map/while/body/eval_jaxpr/kn,snc->skc/dot_general | solution.py:59
  42.9 1.0 convolution_bitcast_fusion.9
  43.9 1.0 convolution_bitcast_fusion.8
  45.0 0.8 multiply_add_fusion.7
  45.8 1.9 %fusion.286 = f32[64,32,256]{2,1,0:T(8,128)S(1)} fusion(f32[64,32,128]{2,1,0:T(8,128)S(1)} %get-tuple-element.512, f32[64,32,128]{2,1,0:T(8,128)S(1)} %get-tuple-element.513, f32[256,256]{1,0:T(8,128)S(1)} %get-tuple-element.544), kind=kOutput, calls=%fused_computation.10.clone.1 | convolution fusion | flops 1611137024 | bytes 4456448 | tf_op jit(solution)/shard_map/while/body/eval_jaxpr/skc,cd->skd/dot_general | solution.py:69
  47.7 1.9 %fusion.287 = f32[64,32,256]{2,1,0:T(8,128)S(1)} fusion(f32[64,32,128]{2,1,0:T(8,128)S(1)} %get-tuple-element.514, f32[64,32,128]{2,1,0:T(8,128)S(1)} %get-tuple-element.515, f32[256,256]{1,0:T(8,128)S(1)} %get-tuple-element.544), kind=kOutput, calls=%fused_computation.5.clone.1 | convolution fusion | flops 1611137024 | bytes 4456448 | tf_op jit(solution)/shard_map/while/body/eval_jaxpr/skc,cd->skd/dot_general | solution.py:69
  49.9 0.8 multiply_add_fusion.8
  51.6 0.7 fusion.289
  52.3 1.3 %dynamic_slice.37 = s32[1]{0:T(128)} dynamic-slice(s32[4]{0:T(128)} %get-tuple-element.542, s32[]{:T(128)S(6)} %copy.37), dynamic_slice_sizes={1} | dynamic-slice | bytes 12 | tf_op jit(solution)/shard_map/while/body/jit(dynamic_index_in_dim)/dynamic_slice | solution.py:147
  53.7 1.1 constant_dynamic-slice_fusion.2
  54.8 1.1 dynamic-slice_convert_fusion.2
  56.1 2.0 %fusion.285 = f32[64,32,256]{2,1,0:T(8,128)S(1)} fusion(f32[64,16,256]{2,1,0:T(8,128)S(1)} %bitcast.89, f32[64,16,256]{2,1,0:T(8,128)S(1)} %bitcast.87), kind=kOutput, calls=%fused_computation.16.clone.1 | convolution fusion | flops 201865216 | bytes 4194304 | tf_op jit(solution)/shard_map/while/body/eval_jaxpr/kn,snc->skc/dot_general | solution.py:58
  58.1 2.0 %fusion.284 = f32[64,32,256]{2,1,0:T(8,128)S(1)} fusion(f32[64,16,256]{2,1,0:T(8,128)S(1)} %bitcast.90, f32[64,16,256]{2,1,0:T(8,128)S(1)} %bitcast.88), kind=kOutput, calls=%fused_computation.17.clone.1 | convolution fusion | flops 201865216 | bytes 4194304 | tf_op jit(solution)/shard_map/while/body/eval_jaxpr/kn,snc->skc/dot_general | solution.py:59
  60.1 1.0 convolution_bitcast_fusion.9
  61.2 1.0 convolution_bitcast_fusion.8
  62.2 0.8 multiply_add_fusion.7
  63.0 1.9 %fusion.286 = f32[64,32,256]{2,1,0:T(8,128)S(1)} fusion(f32[64,32,128]{2,1,0:T(8,128)S(1)} %get-tuple-element.512, f32[64,32,128]{2,1,0:T(8,128)S(1)} %get-tuple-element.513, f32[256,256]{1,0:T(8,128)S(1)} %get-tuple-element.544), kind=kOutput, calls=%fused_computation.10.clone.1 | convolution fusion | flops 1611137024 | bytes 4456448 | tf_op jit(solution)/shard_map/while/body/eval_jaxpr/skc,cd->skd/dot_general | solution.py:69
  64.9 1.9 %fusion.287 = f32[64,32,256]{2,1,0:T(8,128)S(1)} fusion(f32[64,32,128]{2,1,0:T(8,128)S(1)} %get-tuple-element.514, f32[64,32,128]{2,1,0:T(8,128)S(1)} %get-tuple-element.515, f32[256,256]{1,0:T(8,128)S(1)} %get-tuple-element.544), kind=kOutput, calls=%fused_computation.5.clone.1 | convolution fusion | flops 1611137024 | bytes 4456448 | tf_op jit(solution)/shard_map/while/body/eval_jaxpr/skc,cd->skd/dot_general | solution.py:69
  67.1 0.8 multiply_add_fusion.8
  68.8 0.7 fusion.289
  69.7 1.3 %copy.22 = f32[4,2,2048]{0,1,2:T(2,128)S(1)} copy(f32[4,2,2048]{2,0,1:T(4,128)S(1)} %pad_maximum_fusion.11) | data formatting | bytes 131072 | tf_op jit(solution)/shard_map/stack | solution.py:154
  71.0 3.8 %reshape.198 = f32[8,1,2048]{2,1,0:T(1,128)} reshape(f32[2048,2,4]{2,1,0:T(2,128)S(1)} %bitcast.93) | data formatting | bytes 131072
  74.8 7.3 %all-to-all-start = ((f32[8,1,2048]{2,1,0:T(1,128)}), f32[8,1,2048]{2,1,0:T(1,128)S(1)}, u32[]{:S(2)}, u32[]{:S(2)}) async-start(f32[8,1,2048]{2,1,0:T(1,128)} %reshape.198), calls=%async_computation | async-start | bytes 131072 | tf_op jit(solution)/shard_map/all_to_all | solution.py:153
  82.1 0.7 dynamic-slice
  83.7 11.9 %all-reduce.1 = s32[32]{0:T(128)S(1)} all-reduce(s32[32]{0:T(128)S(1)} %dynamic-update-slice), channel_id=1, replica_groups=mesh['tm'=8,'chan'=4] {'tm'}, use_global_device_ids=true, to_apply=%add.1 | all-reduce | flops 32 | bytes 256
  95.6 0.3 fusion.186
  96.2 0.5 broadcast.437
  96.8 0.8 reduce.1
  97.6 3.2 %reshape.199 = f32[2048,2,4]{2,1,0:T(2,128)S(1)} reshape(f32[8,2048]{1,0:T(8,128)S(1)} %reduce.1) | data formatting | bytes 131072
  100.8 0.8 copy.26
  101.8 1.0 fusion.157
  110.6 3.4 %collective-permute-start = (f32[24,512]{1,0:T(8,128)S(1)}, f32[24,512]{1,0:T(8,128)S(1)}, u32[]{:S(2)}, u32[]{:S(2)}) collective-permute-start(f32[24,512]{1,0:T(8,128)S(1)} %get-tuple-element.415), channel_id=1, source_target_pairs={{0,4},{4,8},{8,12},{12,16},{16,20},{20,24},{24,28},{1,5},{5,9},{9,... | collective-permute-start | bytes 147464 | tf_op jit(solution)/shard_map/ppermute | solution.py:25
  114.0 1.5 %collective-permute-start.1 = (f32[24,512]{1,0:T(8,128)S(1)}, f32[24,512]{1,0:T(8,128)S(1)}, u32[]{:S(2)}, u32[]{:S(2)}) collective-permute-start(f32[24,512]{1,0:T(8,128)S(1)} %get-tuple-element.416), channel_id=1, source_target_pairs={{4,0},{8,4},{12,8},{16,12},{20,16},{24,20},{28,24},{5,1},{9,5},{13... | collective-permute-start | bytes 147464 | tf_op jit(solution)/shard_map/ppermute | solution.py:26
  115.7 4.3 %collective-permute-done.1 = f32[24,512]{1,0:T(8,128)S(1)} collective-permute-done((f32[24,512]{1,0:T(8,128)S(1)}, f32[24,512]{1,0:T(8,128)S(1)}, u32[]{:S(2)}, u32[]{:S(2)}) %collective-permute-start.1) | collective-permute-done | bytes 49184 | tf_op jit(solution)/shard_map/ppermute | solution.py:26
  120.0 6.7 %fusion.100 = f32[256,512]{1,0:T(8,128)} fusion(f32[24,512]{1,0:T(8,128)S(1)} %collective-permute-done.1, f32[256,512]{1,0:T(8,128)S(1)} %fusion.106, f32[24,512]{1,0:T(8,128)S(1)} %collective-permute-done, f32[256,1]{1,0:T(8,128)S(1)} %get-tuple-element.412, f32[256,511]{1,0:T(8,128)S(1)} %get-tuple-element.414, f32[256,511]{1,0:T(8,128)S(1)} %get-tuple-element.413, ...), kind=kOutput, calls=%fused_computation.128 | convolution fusion | flops 495104000 | bytes 26342592 | tf_op jit(solution)/shard_map/dot_general | solution.py:175
  (124 shorter events, 14.9 us)
Async XLA Ops:
  69.6 12.4 %copy-start.3 = (u32[32]{0:T(128)S(1)}, u32[32]{0:T(128)}, u32[]{:S(2)}) copy-start(u32[32]{0:T(128)} %constant.235) | copy-start | bytes 388
  69.7 13.8 %copy-start.2 = (s32[4]{0:T(128)S(1)}, s32[4]{0:T(128)}, u32[]{:S(2)}) copy-start(s32[4]{0:T(128)} %param.10) | copy-start | bytes 52
  69.7 25.9 %copy-start = (s32[256]{0:T(256)S(1)}, s32[256]{0:T(256)}, u32[]{:S(2)}) copy-start(s32[256]{0:T(256)} %param.12) | copy-start | bytes 3076
  69.7 25.9 %copy-start.1 = (s32[256]{0:T(256)S(1)}, s32[256]{0:T(256)}, u32[]{:S(2)}) copy-start(s32[256]{0:T(256)} %param.13) | copy-start | bytes 3076
  74.8 21.5 %all-to-all-start = ((f32[8,1,2048]{2,1,0:T(1,128)}), f32[8,1,2048]{2,1,0:T(1,128)S(1)}, u32[]{:S(2)}, u32[]{:S(2)}) async-start(f32[8,1,2048]{2,1,0:T(1,128)} %reshape.198), calls=%async_computation | async-start | bytes 131072 | tf_op jit(solution)/shard_map/all_to_all | solution.py:153
  110.6 5.1 %collective-permute-start = (f32[24,512]{1,0:T(8,128)S(1)}, f32[24,512]{1,0:T(8,128)S(1)}, u32[]{:S(2)}, u32[]{:S(2)}) collective-permute-start(f32[24,512]{1,0:T(8,128)S(1)} %get-tuple-element.415), channel_id=1, source_target_pairs={{0,4},{4,8},{8,12},{12,16},{16,20},{20,24},{24,28},{1,5},{5,9},{9,... | collective-permute-start | bytes 147464 | tf_op jit(solution)/shard_map/ppermute | solution.py:25
  114.0 6.0 %collective-permute-start.1 = (f32[24,512]{1,0:T(8,128)S(1)}, f32[24,512]{1,0:T(8,128)S(1)}, u32[]{:S(2)}, u32[]{:S(2)}) collective-permute-start(f32[24,512]{1,0:T(8,128)S(1)} %get-tuple-element.416), channel_id=1, source_target_pairs={{4,0},{8,4},{12,8},{16,12},{20,16},{24,20},{28,24},{5,1},{9,5},{13... | collective-permute-start | bytes 147464 | tf_op jit(solution)/shard_map/ppermute | solution.py:26
where the time goes:
time: 127 us
  matrix products  50.9 us (40%)
  local copies, waits for them, and re-layouts  28.4 us (22%)
  other arithmetic  17.3 us (14%)
  starting transfers between devices  12.2 us (10%)
  blocking collectives  11.9 us (9%)
  waiting for transfers between devices  4.46 us (4%)
    dot_general x8, matrix products, forward(): return jnp.einsum('skc,cd->skd', turned, mixer, precision=HIGH)  15.2 us
    dot_general x8, matrix products, forward(): second = jnp.einsum('kn,snc->skc', small_sin, signal, precision=HIGH)  12.2 us
    dot_general x8, matrix products, forward(): first = jnp.einsum('kn,snc->skc', small_cos, signal, precision=HIGH)  12.2 us
    unnamed x1, blocking collectives  11.9 us
    dynamic_slice x8, local copies, waits for them, and re-layouts, body(): lax.map(lambda item: correlate(item[0], item[1], item[2], tables), (surve...  9.53 us
    unnamed x15, local copies, waits for them, and re-layouts  7.96 us
    slice x48, local copies, waits for them, and re-layouts, body(): jnp.roll(power, step, axis=1)  7.45 us
    all_to_all x1, starting transfers between devices, body(): lax.all_to_all(jnp.stack([real_c, imag_c], axis=1), 'tm', split_axis=2, c...  7.27 us
  transfers between devices with their start and end apart: 3, of which 2 were waited for; matrix products, arithmetic and copies ran while one was open for 1% of the time, Pallas kernels for 0%

commit v1 on v0

v1 whole, which is shorter than its diff:
```python
import functools
import math

import jax
import jax.numpy as jnp
from jax import lax
from jax.experimental import pallas as pl
from jax.experimental.pallas import tpu as pltpu
from jax.sharding import PartitionSpec as P

D = 2048
DOP = 512
SEGS = 64
GUARD_MAX = 8
WIN_MAX = 16
REACH = GUARD_MAX + WIN_MAX
LANES = 128
LAGS = D // LANES
GROUP = 64

HIGH = lax.Precision.HIGHEST


def correlate_kernel(walk, ids, surv, ref, out, surv_f, ref_f, keys, waves, grams, skewed, natural, *, span):
    step = pl.program_id(0)
    blocks = pl.num_programs(0)
    rows = surv.shape[1]
    members = rows // GROUP
    for half in range(2):
        lanes = slice(half * LANES, (half + 1) * LANES)
        surv_f[half] = surv[0, :, lanes].astype(jnp.float32)
        ref_f[half] = ref[0, :, lanes].astype(jnp.float32)
    for half in range(2):
        lanes = slice(half * LANES, (half + 1) * LANES)
        for sigma in range(0, GROUP, LANES // members):
            tile = jnp.concatenate(
                [surv_f[half, pl.ds(sigma + i, members, stride=GROUP), :] for i in range(LANES // members)], 0
            )
            keys[lanes, sigma * members : sigma * members + LANES] = tile.T.astype(jnp.bfloat16)
        for sigma in range(GROUP + LAGS):
            waves[sigma * members : (sigma + 1) * members, lanes] = ref_f[
                half, pl.ds(sigma, members, stride=GROUP), :
            ].astype(jnp.bfloat16)
    for b in range(LAGS + 1):
        gram = jnp.dot(
            keys[...], waves[b * members : b * members + rows, :], preferred_element_type=jnp.float32
        )
        grams[b, 0] = gram[:LANES, :LANES] + gram[LANES:, LANES:]
        grams[b, 1] = gram[LANES:, :LANES] - gram[:LANES, LANES:]
    sub = lax.broadcasted_iota(jnp.int32, (8, LANES), 0)
    lane = lax.broadcasted_iota(jnp.int32, (8, LANES), 1)
    for b in range(LAGS):
        for part in range(2):
            total = None
            for i in range(LANES // 8):
                own = slice(8 * i, 8 * i + 8)
                mixed = jnp.where(lane > 8 * i + sub, grams[b, part, own], grams[b + 1, part, own])
                if i:
                    mixed = pltpu.roll(mixed, LANES - 8 * i, 1)
                total = mixed if total is None else total + mixed
            at = 8 * (part * LAGS + LAGS - 1 - b)
            skewed[at : at + 8] = total
    summed = None
    for s in range(8):
        line = pltpu.roll(skewed[pl.ds(s, 2 * LAGS, stride=8), :], LANES - s - 1, 1)
        summed = line if summed is None else summed + line
    natural[pl.ds(pl.multiple_of(step * 2 * LAGS, 2 * LAGS), 2 * LAGS), :] = summed

    @pl.when(step == blocks - 1)
    def finish():
        count = natural.shape[0] // (2 * LAGS)
        here = lax.broadcasted_iota(jnp.int32, (LANES, LANES), 0)
        there = lax.broadcasted_iota(jnp.int32, (LANES, LANES), 1)
        flip = (here + there == LANES - 1).astype(jnp.float32)
        delays = jnp.dot(natural[...], flip, precision=HIGH, preferred_element_type=jnp.float32)
        spot = lax.broadcasted_iota(jnp.int32, (LAGS, LANES), 1)
        for row in range(2 * count):
            shift = walk[row // 2]
            moved = pltpu.roll(delays[row * LAGS : (row + 1) * LAGS], shift, 1)
            below = jnp.concatenate([jnp.zeros((1, LANES), jnp.float32), moved[:-1]], 0)
            natural[row * LAGS : (row + 1) * LAGS, :] = jnp.where(spot >= shift, moved, below)
        if span % LANES:
            out[...] = natural[...]
            return
        tiles = span // LANES
        name = jnp.concatenate(
            [jnp.full((1, LANES), ids[row // 2].astype(jnp.float32), jnp.float32) for row in range(2 * count)], 0
        )
        at = lax.broadcasted_iota(jnp.int32, (2 * count, LANES), 1)
        nothing = jnp.zeros((2 * count, LANES), jnp.float32)

        def lag_row(k):
            if k < 0 or k >= LAGS:
                return nothing
            return natural[pl.ds(k, 2 * count, stride=LAGS), :]

        for dest in range(LAGS // tiles):
            for k in range(tiles):
                out[dest, :, k * LANES : (k + 1) * LANES] = lag_row(dest * tiles + k)
            halo = jnp.where(at < 32, lag_row((dest + 1) * tiles), lag_row(dest * tiles - 1))
            out[dest, :, tiles * LANES :] = jnp.where((at >= 32) & (at < 96), name, halo)


def correlate(surveillance, ref_samples, walk, ids, devices):
    blocks, rows, _ = surveillance.shape
    ref_rows = ref_samples.shape[1]
    span = D // devices
    width = window_width(span)
    direct = span % LANES == 0
    shape = (devices, 2 * blocks, width) if direct else (2 * blocks * LAGS, LANES)
    result = pl.pallas_call(
        functools.partial(correlate_kernel, span=span),
        out_shape=jax.ShapeDtypeStruct(shape, jnp.float32),
        grid_spec=pltpu.PrefetchScalarGridSpec(
            num_scalar_prefetch=2,
            grid=(blocks,),
            in_specs=[
                pl.BlockSpec((1, rows, 256), lambda i, *_: (i, 0, 0)),
                pl.BlockSpec((1, ref_rows, 256), lambda i, *_: (i, 0, 0)),
            ],
            out_specs=pl.BlockSpec(shape, lambda i, *_: (0,) * len(shape)),
            scratch_shapes=[
                pltpu.VMEM((2, rows, LANES), jnp.float32),
                pltpu.VMEM((2, ref_rows, LANES), jnp.float32),
                pltpu.VMEM((256, rows), jnp.bfloat16),
                pltpu.VMEM((rows + LAGS * (rows // GROUP), 256), jnp.bfloat16),
                pltpu.VMEM((LAGS + 1, 2, LANES, LANES), jnp.float32),
                pltpu.VMEM((2 * LAGS * 8, LANES), jnp.float32),
                pltpu.VMEM((2 * blocks * LAGS, LANES), jnp.float32),
            ],
        ),
        compiler_params=pltpu.CompilerParams(dimension_semantics=("arbitrary",)),
    )(walk, ids, surveillance, ref_samples)
    if direct:
        return result
    flat = result.reshape(2 * blocks, D)
    names = jnp.repeat(ids.astype(jnp.float32), 2)[:, None]
    padded = jnp.pad(flat, ((0, 0), (REACH, REACH)))
    fill = jnp.broadcast_to(names, (2 * blocks, width - span - 2 * REACH))
    return jnp.stack(
        [
            jnp.concatenate(
                [
                    padded[:, p * span + REACH : (p + 1) * span + 2 * REACH],
                    fill,
                    padded[:, p * span : p * span + REACH],
                ],
                1,
            )
            for p in range(devices)
        ]
    )


def window_width(span):
    return -(-(span + 2 * REACH + 16) // LANES) * LANES


def split(x):
    top = x.astype(jnp.bfloat16)
    return top, (x - top.astype(jnp.float32)).astype(jnp.bfloat16)


def cosine(turn):
    turn = turn & (DOP - 1)
    turn = jnp.minimum(turn, DOP - turn)
    x = (DOP // 4 - turn).astype(jnp.float32) * (2.0 * math.pi / DOP)
    y = x * x
    poly = 1.0
    for n in (13, 11, 9, 7, 5, 3):
        poly = 1.0 - y * poly * (1.0 / (n * (n - 1)))
    return x * poly


def detect_kernel(base, moved, cells, out, power, delay, sizes, *, norm):
    span = out.shape[0]
    sources, lines, width = moved.shape
    stacked = moved[...].reshape(sources * lines, width)
    count = sources * lines
    ids = stacked[:, span + 32 : span + 33].astype(jnp.int32)
    freq = lax.broadcasted_iota(jnp.int32, (count, DOP), 1)
    imag = lax.broadcasted_iota(jnp.int32, (count, DOP), 0) & 1
    turn = ids * freq - imag * (DOP // 4)
    mixer = jnp.concatenate([cosine(turn), cosine(turn + DOP // 4)], 1)
    top, rest = split(stacked * norm)
    mix_top, mix_rest = split(mixer)
    amp = lax.dot_general(
        jnp.concatenate([top, top, rest], 0),
        jnp.concatenate([mix_top, mix_rest, mix_top], 0),
        (((0,), (0,)), ((), ())),
        preferred_element_type=jnp.float32,
    )
    whole = amp[:, :DOP] * amp[:, :DOP] + amp[:, DOP:] * amp[:, DOP:]
    power[...] = whole[:span]
    tile = cells.shape[1]
    for k in range(cells.shape[0]):
        spread = jnp.broadcast_to(cells[k : k + 1, :].astype(jnp.float32), (tile, tile)).T
        sizes[k * tile : (k + 1) * tile, :] = spread[:, :1].astype(jnp.int32)
    packed = sizes[...]
    guard = packed & 31
    reach = guard + (packed >> 5)
    place = lax.broadcasted_iota(jnp.int32, (span, width), 1)
    place = jnp.where(place < span + 32, place, place - width)
    dist = jnp.abs(place - lax.broadcasted_iota(jnp.int32, (span, width), 0))
    spot = place + base[0]
    band = (dist > guard) & (dist <= reach) & (spot >= 0) & (spot < D)
    band = jnp.where(band, 1.0, 0.0)
    tally = jnp.sum(band, axis=1, keepdims=True)
    band = band.astype(jnp.bfloat16)
    top, rest = split(whole)
    delay[...] = (
        jnp.dot(band, top, preferred_element_type=jnp.float32)
        + jnp.dot(band, rest, preferred_element_type=jnp.float32)
    )
    weight = 1.0 / (tally + 2.0 * (reach - guard).astype(jnp.float32))
    rows = 16
    for k in range(span // rows):
        own = slice(k * rows, (k + 1) * rows)
        cell = power[own]
        low = guard[own]
        high = reach[own]
        wide = high - low

        def ahead(x, n):
            return pltpu.roll(x, DOP - n, 1)

        sums = [cell]
        for e in range(4):
            sums.append(sums[-1] + ahead(sums[-1], 1 << e))
        near = jnp.where((wide & 16) > 0, sums[4], 0.0)
        for e in (3, 2, 1, 0):
            near = jnp.where((wide & (1 << e)) > 0, sums[e] + ahead(near, 1 << e), near)
        right = near
        for e in range(4):
            right = jnp.where(((low + 1) & (1 << e)) > 0, ahead(right, 1 << e), right)
        left = near
        for e in range(5):
            left = jnp.where((high & (1 << e)) > 0, pltpu.roll(left, 1 << e, 1), left)
        level = jnp.sum(cell, axis=1, keepdims=True) * (1.0 / DOP)
        noise = (delay[own] + left + right) * weight[own]
        out[own] = (cell - level) / (0.25 + noise)


def detect(moved, base, guard, window, norm):
    span = guard.shape[0]
    width = moved.shape[2]
    tile = min(span, LANES)
    cells = (guard + 32 * window).reshape(span // tile, tile)
    whole = pl.BlockSpec(memory_space=pltpu.VMEM)
    return pl.pallas_call(
        functools.partial(detect_kernel, norm=norm),
        out_shape=jax.ShapeDtypeStruct((span, DOP), jnp.float32),
        in_specs=[pl.BlockSpec(memory_space=pltpu.SMEM), whole, whole],
        out_specs=whole,
        scratch_shapes=[
            pltpu.VMEM((span, DOP), jnp.float32),
            pltpu.VMEM((span, DOP), jnp.float32),
            pltpu.VMEM((span, 1), jnp.int32),
        ],
    )(base, moved, cells)


def body(surveillance, ref_samples, block_ids, walk, cfar_guard, cfar_window):
    blocks = surveillance.shape[0]
    devices = lax.axis_size("tm")
    norm = 1.0 / math.sqrt(blocks * devices * SEGS * D)
    windows = correlate(surveillance, ref_samples, walk, block_ids, devices)
    moved = lax.all_to_all(windows, "tm", split_axis=0, concat_axis=0, tiled=True)
    base = (lax.axis_index("tm") * (D // devices)).astype(jnp.int32).reshape(1)
    return detect(moved, base, cfar_guard, cfar_window, norm)


def solution(mesh):
    in_specs = (
        P(("chan", "tm"), None, None),
        P("tm", None, None),
        P("tm"),
        P("tm"),
        P("tm"),
        P("tm"),
    )
    out_specs = P(("chan", "tm"), None)
    return jax.shard_map(body, mesh=mesh, in_specs=in_specs, out_specs=out_specs, check_vma=False)
```

time: 127 us -> 51.1 us (0.40)
  matrix products: 50.9 us -> 0 us
  Pallas kernels: 0 us -> 35.8 us
  local copies, waits for them, and re-layouts: 28.4 us -> 0.64 us
  other arithmetic: 17.3 us -> 0.55 us
  blocking collectives: 11.9 us -> 0 us
  starting transfers between devices: 12.2 us -> 7.28 us
  waiting for transfers between devices: 4.46 us -> 6.56 us
    dot_general x39 -> x0, matrix products: 50.9 us -> none  [the longest x8 15.2 us: forward(): return jnp.einsum('skc,cd->skd', turned, mixer, precision=HIGH)]
    pallas_call x0 -> x2, Pallas kernels: none -> 35.8 us  [the longest x1 19.2 us: correlate(): pl.pallas_call(functools.partial(correlate_kernel, span=span), out_shape=...]
    unnamed x1 -> x0, blocking collectives: 11.9 us -> none
    dynamic_slice x8 -> x0, local copies, waits for them, and re-layouts: 9.53 us -> none  [body(): lax.map(lambda item: correlate(item[0], item[1], item[2], tables), (surve...]
    slice x55 -> x0, local copies, waits for them, and re-layouts: 8.18 us -> none  [the longest x48 7.45 us: body(): jnp.roll(power, step, axis=1)]
    unnamed x15 -> x6, local copies, waits for them, and re-layouts: 7.96 us -> 0.64 us
    all_to_all x1, waiting for transfers between devices: 0.01 us -> 6.56 us  [body(): lax.all_to_all(windows, 'tm', split_axis=0, concat_axis=0, tiled=True)]
    add x10 -> x0, other arithmetic: 6.21 us -> none  [the longest x4 3.06 us: forward(): real_part * twist_cos + imag_part * twist_sin]
  transfers between devices with their start and end apart: 3 -> 1, of which waited for: 2 -> 1; matrix products, arithmetic and copies ran while one was open for 1% -> 1% of each run, Pallas kernels for 0% -> 0%
where the time goes in v1:
time: 51.1 us; the launch traced here: 50.9 us
  Pallas kernels  35.8 us (70%)
  starting transfers between devices  7.28 us (14%)
  waiting for transfers between devices  6.56 us (13%)
  local copies, waits for them, and re-layouts  0.64 us (1%)
  other arithmetic  0.55 us (1%)
    pallas_call x1, Pallas kernels, correlate(): pl.pallas_call(functools.partial(correlate_kernel, span=span), out_shape=...  19.2 us
    pallas_call x1, Pallas kernels, detect(): pl.pallas_call(functools.partial(detect_kernel, norm=norm), out_shape=jax...  16.6 us
    all_to_all x1, starting transfers between devices, body(): lax.all_to_all(windows, 'tm', split_axis=0, concat_axis=0, tiled=True)  7.28 us
    all_to_all x1, waiting for transfers between devices, body(): lax.all_to_all(windows, 'tm', split_axis=0, concat_axis=0, tiled=True)  6.56 us
  transfers between devices with their start and end apart: 1, of which 1 were waited for; matrix products, arithmetic and copies ran while one was open for 1% of the time, Pallas kernels for 0%

profile of v1, /device:TPU:0, one launch (start us, length us, event | category | flops | bytes accessed | tf_op | source)
XLA Modules:
  0.0 50.9 jit_solution(1399705197331330459)
XLA Ops:
  0.0 0.0 copy-start.2
  0.0 0.0 copy-start.1
  0.0 19.2 %shard_map.64 = f32[8,8,384]{2,1,0:T(8,128)} custom-call(s32[4]{0:T(128)} %walk.1, s32[4]{0:T(128)} %ids.1, bf16[4,1024,256]{2,1,0:T(8,128)(2,1)} %surv.1, bf16[4,1040,256]{2,1,0:T(8,128)(2,1)} %ref.1), custom_call_target="tpu_custom_call" | custom-call | tf_op jit(solution)/shard_map/pallas_call | solution.py:111
  19.2 7.3 %all-to-all-start = ((f32[8,8,384]{2,1,0:T(8,128)}), f32[8,8,384]{2,1,0:T(8,128)S(1)}, u32[]{:S(2)}, u32[]{:S(2)}) async-start(f32[8,8,384]{2,1,0:T(8,128)} %shard_map.64), calls=%async_computation | async-start | bytes 196608 | tf_op jit(solution)/shard_map/all_to_all | solution.py:268
  26.5 0.0 copy-done.2
  26.5 0.0 copy-done.1
  26.5 0.5 %add_bitcast_fusion.cells = s32[2,128]{1,0:T(2,128)} fusion(s32[256]{0:T(256)S(1)} %copy-done.1, s32[256]{0:T(256)S(1)} %copy-done.2), kind=kLoop, calls=%fused_computation | loop fusion | flops 512 | bytes 3072 | tf_op jit(solution)/shard_map/reshape | solution.py:248
  27.0 6.6 %all-to-all-done.moved = f32[8,8,384]{2,1,0:T(8,128)S(1)} async-done(((f32[8,8,384]{2,1,0:T(8,128)}), f32[8,8,384]{2,1,0:T(8,128)S(1)}, u32[]{:S(2)}, u32[]{:S(2)}) %all-to-all-start) | async-done | bytes 98336 | tf_op jit(solution)/shard_map/all_to_all | solution.py:268
  33.6 0.0 copy-start
  33.6 0.6 %copy-done = f32[8,8,384]{2,1,0:T(8,128)} copy-done((f32[8,8,384]{2,1,0:T(8,128)}, f32[8,8,384]{2,1,0:T(8,128)S(1)}, u32[]{:S(2)}) %copy-start) | copy-done | bytes 98328
  34.2 16.6 %shard_map.65 = f32[256,512]{1,0:T(8,128)} custom-call(s32[1]{0:T(128)} %bitcast.base, f32[8,8,384]{2,1,0:T(8,128)} %copy-done, s32[2,128]{1,0:T(2,128)} %add_bitcast_fusion.cells), custom_call_target="tpu_custom_call" | custom-call | tf_op jit(solution)/shard_map/pallas_call | solution.py:250
Async XLA Ops:
  0.0 26.5 %copy-start.2 = (s32[256]{0:T(256)S(1)}, s32[256]{0:T(256)}, u32[]{:S(2)}) copy-start(s32[256]{0:T(256)} %param.11) | copy-start | bytes 3076
  0.0 26.5 %copy-start.1 = (s32[256]{0:T(256)S(1)}, s32[256]{0:T(256)}, u32[]{:S(2)}) copy-start(s32[256]{0:T(256)} %param.10) | copy-start | bytes 3076
  19.2 14.4 %all-to-all-start = ((f32[8,8,384]{2,1,0:T(8,128)}), f32[8,8,384]{2,1,0:T(8,128)S(1)}, u32[]{:S(2)}, u32[]{:S(2)}) async-start(f32[8,8,384]{2,1,0:T(8,128)} %shard_map.64), calls=%async_computation | async-start | bytes 196608 | tf_op jit(solution)/shard_map/all_to_all | solution.py:268
  33.6 0.6 %copy-start = (f32[8,8,384]{2,1,0:T(8,128)}, f32[8,8,384]{2,1,0:T(8,128)S(1)}, u32[]{:S(2)}) copy-start(f32[8,8,384]{2,1,0:T(8,128)S(1)} %all-to-all-done.moved) | copy-start | bytes 294916

commit v2 on v1

--- a/solution.py
+++ b/solution.py
@@ -16,7 +16,7 @@
 REACH = GUARD_MAX + WIN_MAX
 LANES = 128
 LAGS = D // LANES
-GROUP = 64
+GROUP = 8
 
 HIGH = lax.Precision.HIGHEST
 
@@ -172,73 +172,70 @@
     return x * poly
 
 
-def detect_kernel(base, moved, cells, out, power, delay, sizes, *, norm):
+def detect_kernel(base, moved, cells, out, *, norm):
     span = out.shape[0]
     sources, lines, width = moved.shape
-    stacked = moved[...].reshape(sources * lines, width)
     count = sources * lines
-    ids = stacked[:, span + 32 : span + 33].astype(jnp.int32)
-    freq = lax.broadcasted_iota(jnp.int32, (count, DOP), 1)
-    imag = lax.broadcasted_iota(jnp.int32, (count, DOP), 0) & 1
-    turn = ids * freq - imag * (DOP // 4)
-    mixer = jnp.concatenate([cosine(turn), cosine(turn + DOP // 4)], 1)
-    top, rest = split(stacked * norm)
-    mix_top, mix_rest = split(mixer)
-    amp = lax.dot_general(
-        jnp.concatenate([top, top, rest], 0),
-        jnp.concatenate([mix_top, mix_rest, mix_top], 0),
-        (((0,), (0,)), ((), ())),
+    stacked = moved[...].reshape(count, width)
+    names = stacked[:, width - LANES :]
+    names = jnp.concatenate([names, names], 0).T
+    at = span + 32 - (width - LANES)
+    ids = names[at : at + 1, :].astype(jnp.int32)
+    freq = lax.broadcasted_iota(jnp.int32, (DOP, 2 * count), 0)
+    imag = lax.broadcasted_iota(jnp.int32, (DOP, 2 * count), 1) & 1
+    mix_top, mix_rest = split(cosine(ids * freq - imag * (DOP // 4)))
+    stacked = stacked * norm
+    even = lax.broadcasted_iota(jnp.int32, (count, width), 0) & 1 == 0
+    turned = jnp.where(even, pltpu.roll(stacked, count - 1, 0), -pltpu.roll(stacked, 1, 0))
+    top, rest = split(jnp.concatenate([stacked, turned], 1))
+    amp = jnp.dot(
+        jnp.concatenate([mix_top, mix_rest], 1),
+        jnp.concatenate([top, rest, top, rest], 0),
         preferred_element_type=jnp.float32,
     )
-    whole = amp[:, :DOP] * amp[:, :DOP] + amp[:, DOP:] * amp[:, DOP:]
-    power[...] = whole[:span]
+    whole = amp[:, :width] * amp[:, :width] + amp[:, width:] * amp[:, width:]
+    top, rest = split(whole)
     tile = cells.shape[1]
     for k in range(cells.shape[0]):
-        spread = jnp.broadcast_to(cells[k : k + 1, :].astype(jnp.float32), (tile, tile)).T
-        sizes[k * tile : (k + 1) * tile, :] = spread[:, :1].astype(jnp.int32)
-    packed = sizes[...]
-    guard = packed & 31
-    reach = guard + (packed >> 5)
-    place = lax.broadcasted_iota(jnp.int32, (span, width), 1)
-    place = jnp.where(place < span + 32, place, place - width)
-    dist = jnp.abs(place - lax.broadcasted_iota(jnp.int32, (span, width), 0))
-    spot = place + base[0]
-    band = (dist > guard) & (dist <= reach) & (spot >= 0) & (spot < D)
-    band = jnp.where(band, 1.0, 0.0)
-    tally = jnp.sum(band, axis=1, keepdims=True)
-    band = band.astype(jnp.bfloat16)
-    top, rest = split(whole)
-    delay[...] = (
-        jnp.dot(band, top, preferred_element_type=jnp.float32)
-        + jnp.dot(band, rest, preferred_element_type=jnp.float32)
-    )
-    weight = 1.0 / (tally + 2.0 * (reach - guard).astype(jnp.float32))
-    rows = 16
-    for k in range(span // rows):
-        own = slice(k * rows, (k + 1) * rows)
-        cell = power[own]
-        low = guard[own]
-        high = reach[own]
-        wide = high - low
+        packed = cells[k : k + 1, :]
+        low = packed & 31
+        wide = packed >> 5
+        high = low + wide
+        place = lax.broadcasted_iota(jnp.int32, (width, tile), 0)
+        place = jnp.where(place < span + 32, place, place - width)
+        dist = jnp.abs(place - k * tile - lax.broadcasted_iota(jnp.int32, (width, tile), 1))
+        spot = place + base[0]
+        band = (dist > low) & (dist <= high) & (spot >= 0) & (spot < D)
+        band = jnp.where(band, 1.0, 0.0)
+        tally = jnp.sum(band, axis=0, keepdims=True)
+        band = band.astype(jnp.bfloat16)
+        delay = jnp.dot(top, band, preferred_element_type=jnp.float32) + jnp.dot(
+            rest, band, preferred_element_type=jnp.float32
+        )
+        weight = 1.0 / (tally + 2.0 * wide.astype(jnp.float32))
+        cell = whole[:, k * tile : (k + 1) * tile]
 
         def ahead(x, n):
-            return pltpu.roll(x, DOP - n, 1)
+            return pltpu.roll(x, DOP - n, 0)
+
+        def has(x, e):
+            return (x & (1 << e)) > 0
 
         sums = [cell]
         for e in range(4):
             sums.append(sums[-1] + ahead(sums[-1], 1 << e))
-        near = jnp.where((wide & 16) > 0, sums[4], 0.0)
+        near = jnp.where(has(wide, 4), sums[4], 0.0)
         for e in (3, 2, 1, 0):
-            near = jnp.where((wide & (1 << e)) > 0, sums[e] + ahead(near, 1 << e), near)
+            near = jnp.where(has(wide, e), sums[e] + ahead(near, 1 << e), near)
         right = near
         for e in range(4):
-            right = jnp.where(((low + 1) & (1 << e)) > 0, ahead(right, 1 << e), right)
+            right = jnp.where(has(low + 1, e), ahead(right, 1 << e), right)
         left = near
         for e in range(5):
-            left = jnp.where((high & (1 << e)) > 0, pltpu.roll(left, 1 << e, 1), left)
-        level = jnp.sum(cell, axis=1, keepdims=True) * (1.0 / DOP)
-        noise = (delay[own] + left + right) * weight[own]
-        out[own] = (cell - level) / (0.25 + noise)
+            left = jnp.where(has(high, e), pltpu.roll(left, 1 << e, 0), left)
+        level = jnp.sum(cell, axis=0, keepdims=True) * (1.0 / DOP)
+        noise = (delay + left + right) * weight
+        out[k * tile : (k + 1) * tile, :] = ((cell - level) / (0.25 + noise)).T
 
 
 def detect(moved, base, guard, window, norm):
@@ -252,11 +249,6 @@
         out_shape=jax.ShapeDtypeStruct((span, DOP), jnp.float32),
         in_specs=[pl.BlockSpec(memory_space=pltpu.SMEM), whole, whole],
         out_specs=whole,
-        scratch_shapes=[
-            pltpu.VMEM((span, DOP), jnp.float32),
-            pltpu.VMEM((span, DOP), jnp.float32),
-            pltpu.VMEM((span, 1), jnp.int32),
-        ],
     )(base, moved, cells)
 
 

time: 51.1 us -> 35.7 us (0.70)
  Pallas kernels: 35.8 us -> 20.4 us
    pallas_call x1, Pallas kernels: 16.6 us -> 3.74 us  [detect(): pl.pallas_call(functools.partial(detect_kernel, norm=norm), out_shape=jax...]
    pallas_call x1, Pallas kernels: 19.2 us -> 16.7 us  [correlate(): pl.pallas_call(functools.partial(correlate_kernel, span=span), out_shape=...]
  transfers between devices with their start and end apart: 1 -> 1, of which waited for: 1 -> 1; matrix products, arithmetic and copies ran while one was open for 1% -> 2% of each run, Pallas kernels for 0% -> 0%
where the time goes in v2:
time: 35.7 us; the launch traced here: 35.5 us
  Pallas kernels  20.4 us (57%)
  starting transfers between devices  7.28 us (20%)
  waiting for transfers between devices  6.56 us (18%)
  local copies, waits for them, and re-layouts  0.64 us (2%)
  other arithmetic  0.55 us (2%)
    pallas_call x1, Pallas kernels, correlate(): pl.pallas_call(functools.partial(correlate_kernel, span=span), out_shape=...  16.7 us
    all_to_all x1, starting transfers between devices, body(): lax.all_to_all(windows, 'tm', split_axis=0, concat_axis=0, tiled=True)  7.28 us
    all_to_all x1, waiting for transfers between devices, body(): lax.all_to_all(windows, 'tm', split_axis=0, concat_axis=0, tiled=True)  6.56 us
    pallas_call x1, Pallas kernels, detect(): pl.pallas_call(functools.partial(detect_kernel, norm=norm), out_shape=jax...  3.74 us
  transfers between devices with their start and end apart: 1, of which 1 were waited for; matrix products, arithmetic and copies ran while one was open for 2% of the time, Pallas kernels for 0%

profile of v2, /device:TPU:0, one launch (start us, length us, event | category | flops | bytes accessed | tf_op | source)
XLA Modules:
  0.0 35.5 jit_solution(7413792812698863809)
XLA Ops:
  0.0 0.0 copy-start.2
  0.0 0.0 copy-start.1
  0.0 16.7 %shard_map.64 = f32[8,8,384]{2,1,0:T(8,128)} custom-call(s32[4]{0:T(128)} %walk.1, s32[4]{0:T(128)} %ids.1, bf16[4,1024,256]{2,1,0:T(8,128)(2,1)} %surv.1, bf16[4,1040,256]{2,1,0:T(8,128)(2,1)} %ref.1), custom_call_target="tpu_custom_call" | custom-call | tf_op jit(solution)/shard_map/pallas_call | solution.py:111
  16.7 7.3 %all-to-all-start = ((f32[8,8,384]{2,1,0:T(8,128)}), f32[8,8,384]{2,1,0:T(8,128)S(1)}, u32[]{:S(2)}, u32[]{:S(2)}) async-start(f32[8,8,384]{2,1,0:T(8,128)} %shard_map.64), calls=%async_computation | async-start | bytes 196608 | tf_op jit(solution)/shard_map/all_to_all | solution.py:260
  24.0 0.0 copy-done.2
  24.0 0.0 copy-done.1
  24.0 0.5 %add_bitcast_fusion.cells = s32[2,128]{1,0:T(2,128)} fusion(s32[256]{0:T(256)S(1)} %copy-done.1, s32[256]{0:T(256)S(1)} %copy-done.2), kind=kLoop, calls=%fused_computation | loop fusion | flops 512 | bytes 3072 | tf_op jit(solution)/shard_map/reshape | solution.py:245
  24.5 6.6 %all-to-all-done.moved = f32[8,8,384]{2,1,0:T(8,128)S(1)} async-done(((f32[8,8,384]{2,1,0:T(8,128)}), f32[8,8,384]{2,1,0:T(8,128)S(1)}, u32[]{:S(2)}, u32[]{:S(2)}) %all-to-all-start) | async-done | bytes 98336 | tf_op jit(solution)/shard_map/all_to_all | solution.py:260
  31.1 0.0 copy-start
  31.1 0.6 %copy-done = f32[8,8,384]{2,1,0:T(8,128)} copy-done((f32[8,8,384]{2,1,0:T(8,128)}, f32[8,8,384]{2,1,0:T(8,128)S(1)}, u32[]{:S(2)}) %copy-start) | copy-done | bytes 98328
  31.7 3.7 %shard_map.65 = f32[256,512]{1,0:T(8,128)} custom-call(s32[1]{0:T(128)} %bitcast.base, f32[8,8,384]{2,1,0:T(8,128)} %copy-done, s32[2,128]{1,0:T(2,128)} %add_bitcast_fusion.cells), custom_call_target="tpu_custom_call" | custom-call | tf_op jit(solution)/shard_map/pallas_call | solution.py:247
Async XLA Ops:
  0.0 24.0 %copy-start.2 = (s32[256]{0:T(256)S(1)}, s32[256]{0:T(256)}, u32[]{:S(2)}) copy-start(s32[256]{0:T(256)} %param.11) | copy-start | bytes 3076
  0.0 24.0 %copy-start.1 = (s32[256]{0:T(256)S(1)}, s32[256]{0:T(256)}, u32[]{:S(2)}) copy-start(s32[256]{0:T(256)} %param.10) | copy-start | bytes 3076
  16.7 14.4 %all-to-all-start = ((f32[8,8,384]{2,1,0:T(8,128)}), f32[8,8,384]{2,1,0:T(8,128)S(1)}, u32[]{:S(2)}, u32[]{:S(2)}) async-start(f32[8,8,384]{2,1,0:T(8,128)} %shard_map.64), calls=%async_computation | async-start | bytes 196608 | tf_op jit(solution)/shard_map/all_to_all | solution.py:260
  31.1 0.6 %copy-start = (f32[8,8,384]{2,1,0:T(8,128)}, f32[8,8,384]{2,1,0:T(8,128)S(1)}, u32[]{:S(2)}) copy-start(f32[8,8,384]{2,1,0:T(8,128)S(1)} %all-to-all-done.moved) | copy-start | bytes 294916
